TPU v7x, 32 devices: a whole 2x2x4 slice. The times are simulated.
32 devices in a mesh: tab: 2 (over x), cand: 4 (over z), dp: 4 (over y, core).
Axes of the slice: x: 2, y: 2, z: 4, core: 2. Of those that a mesh axis runs over, the one named last changes fastest.
Arguments:
- tables: bfloat16 [16, 65536, 128], P(('cand', 'dp'), 'tab'), may hold values from -6 to 6
- bag_ids: int32 [16, 1024, 16], P(('cand', 'dp')), may hold values from 0 to 65535
- bag_lengths: int32 [16, 1024], P(('cand', 'dp')), may hold values from 1 to 16
- item_weight: bfloat16 [2048, 256], replicated, may hold values from -0.125 to 0.125
- user_features: bfloat16 [16384, 512], P(('tab', 'dp')), may hold values from -6 to 6
- user_w1: bfloat16 [512, 1024], replicated, may hold values from -0.25 to 0.25
- user_w2: bfloat16 [1024, 256], replicated, may hold values from -0.1875 to 0.1875
- positive_items: int32 [16384], P(('tab', 'dp')), may hold values from 0 to 1023
Outputs:
- item_emb: float32 [1024, 256], P(('tab', 'cand', 'dp'))
- user_loss: float32 [16384], P(('tab', 'dp'))
Inputs may be any that keep to these rules, and one draw needn't show every extreme that they name: `bag_ids`: row ids of a table. Only the first bag_lengths ids of a bag count; the rest is padding.
All inputs are finite; a program needn't handle non-finite values.
Results may differ from a plain program's by a relative error of at most 0.00046.
Values sent between devices are 32-bit elements; how exact they have to be, the bound alone decides.
A program may use at most 64 MiB of HBM per device.

v0:
```python
import functools
import math

import jax
import jax.numpy as jnp
from jax import lax
from jax.experimental import pallas as pl
from jax.experimental.pallas import tpu as pltpu
from jax.sharding import PartitionSpec as P

epsilon = 1e-06
logit_scale = 20.0
MESH = pl.DeviceIdType.MESH
F32 = jnp.float32
BF16 = jnp.bfloat16
VMEM_LIMIT = 60 * 1024 * 1024


def split3(x):
    hi = x.astype(BF16)
    rest = x - hi.astype(F32)
    mid = rest.astype(BF16)
    lo = (rest - mid.astype(F32)).astype(BF16)
    return hi, mid, lo


def split2(x):
    hi = x.astype(BF16)
    return hi, (x - hi.astype(F32)).astype(BF16)


def unit_rows(vectors):
    return vectors * lax.rsqrt(jnp.mean(vectors * vectors, axis=-1, keepdims=True) + epsilon)


def dot(a, b):
    return jnp.dot(a, b, preferred_element_type=F32)


def main_kernel(
    sizes,
    length,
    *refs,
):
    ids, refs = refs[:length], refs[length:]
    run_step(sizes, ids, *refs)


def run_step(
    sizes,
    ids,
    inverse,
    table,
    weight_in,
    features_in,
    w1_in,
    w2_in,
    positives,
    emb_out,
    loss_out,
    narrow,
    wide,
    weight,
    features,
    w1,
    w2,
    pooled,
    arrived,
    joined,
    acc,
    user_hi,
    user_lo,
    gathered,
    items_flat,
    sums_here,
    sums_all,
    load_sems,
    table_sems,
    send_a,
    recv_a,
    send_b,
    recv_b,
    send_c,
    recv_c,
):
    num_tab, num_cand, num_dp = sizes
    total = num_tab * num_cand * num_dp
    groups = num_cand * num_dp
    t, c, d = (lax.axis_index(n) for n in ("tab", "cand", "dp"))
    me = (t * num_cand + c) * num_dp + d
    per_block, width = pooled.shape[1:]
    items = total * per_block
    rows, _ = table.shape
    users = features.shape[0]
    hidden = w1.shape[1]
    embed = w2.shape[1]
    tile = acc.shape[0]
    part_width = min(hidden, 256)
    parts = hidden // part_width
    tiles = users // tile
    chunks = table_sems.shape[0]
    steps = (tiles - chunks) * parts
    blocks_step = total // steps
    items_step = items // steps
    chunk = rows // chunks

    def place(index):
        return (index // groups, index // num_dp % num_cand, index % num_dp)

    barrier = pltpu.get_barrier_semaphore()

    @pl.loop(1, total)
    def _(j):
        peer = lax.rem(me + j, total)
        pl.semaphore_signal(barrier, inc=1, device_id=place(peer), device_id_type=MESH)

    loads = [
        pltpu.make_async_copy(a, b, load_sems.at[i])
        for i, (a, b) in enumerate(
            ((w1_in, w1), (w2_in, w2), (features_in, features), (weight_in, weight))
        )
    ]

    def chunk_copy(n):
        part = pl.ds(pl.multiple_of(n * chunk, chunk), chunk)
        return pltpu.make_async_copy(table.at[part], narrow.at[part], table_sems.at[n])

    for load in loads[:3]:
        load.start()
    for n in range(chunks):
        chunk_copy(n).start()
    loads[3].start()
    wide[pl.ds(rows, 8), :] = jnp.zeros((8, width), F32)
    for load in loads[:3]:
        load.wait()

    def tower_part(x, w1_part, w2_part):
        z = dot(x, w1_part)
        z = z * (0.5 * lax.erf(z * math.sqrt(0.5)) + 0.5)
        return dot(z.astype(BF16), w2_part)

    def keep_user(user_rows, pre):
        hi, lo = split2(unit_rows(pre) * (logit_scale / embed))
        user_hi[user_rows, :] = hi
        user_lo[user_rows, :] = lo

    @pl.loop(0, chunks)
    def _(n):
        user_rows = pl.ds(pl.multiple_of(n * tile, tile), tile)
        chunk_copy(n).wait()
        part = pl.ds(pl.multiple_of(n * chunk, chunk), chunk)
        wide[part, :] = narrow[part, :].astype(F32)
        x = features[user_rows, :]
        pre = None
        for h in range(0, hidden, part_width):
            term = tower_part(x, w1[:, h : h + part_width], w2[h : h + part_width, :])
            pre = term if pre is None else pre + term
        keep_user(user_rows, pre)

    pl.semaphore_wait(barrier, total - 1)

    def send(dest):
        pltpu.make_async_remote_copy(
            src_ref=pooled.at[dest],
            dst_ref=arrived.at[me],
            send_sem=send_a,
            recv_sem=recv_a,
            device_id=place(dest),
            device_id_type=MESH,
        ).start()

    my_group = me // blocks_step

    @pl.loop(0, steps)
    def _(s):
        @pl.when(s > 0)
        def _():
            before = lax.rem(my_group + s, steps)
            for i in range(blocks_step):
                send(before * blocks_step + i)

        group = lax.rem(my_group + 1 + s, steps)
        first = group * items_step
        for k in range(items_step):
            terms = [wide[pl.ds(of_place[first + k], 1), :] for of_place in ids]
            while len(terms) > 1:
                terms = [a + b for a, b in zip(terms[::2], terms[1::2])] + (
                    [terms[-1]] if len(terms) % 2 else []
                )
            row = terms[0] * inverse[first + k]
            pooled[group * blocks_step + k // per_block, pl.ds(k % per_block, 1), :] = row

        piece = lax.rem(s, parts)
        user_rows = pl.ds(pl.multiple_of((chunks + s // parts) * tile, tile), tile)
        cols = pl.ds(pl.multiple_of(piece * part_width, part_width), part_width)
        term = tower_part(features[user_rows, :], w1[:, cols], w2[cols, :])
        acc[...] = jnp.where(piece == 0, jnp.zeros_like(term), acc[...]) + term

        @pl.when(piece == parts - 1)
        def _():
            keep_user(user_rows, acc[...])

    for i in range(blocks_step):
        dest = my_group * blocks_step + i
        if blocks_step > 1:

            @pl.when(dest != me)
            def _():
                send(dest)

    arrived[me] = pooled[me]
    loads[3].wait()
    others = pl.ds(0, total - 1)
    pltpu.make_async_copy(arrived.at[others], arrived.at[others], recv_a).wait()
    for f in range(groups):
        block = arrived[f]
        for s in range(1, num_tab):
            block = block + arrived[s * groups + f]
        joined[:, f * width : (f + 1) * width] = block
    hi, mid, lo = split3(joined[...])
    w = weight[...]
    item_emb = unit_rows(dot(lo, w) + dot(mid, w) + dot(hi, w))
    emb_out[...] = item_emb

    slots = num_tab * num_dp
    my_slot = t * num_dp + d

    @pl.loop(1, slots)
    def _(j):
        slot = lax.rem(my_slot + j, slots)
        pltpu.make_async_remote_copy(
            src_ref=emb_out,
            dst_ref=gathered.at[my_slot],
            send_sem=send_b,
            recv_sem=recv_b,
            device_id=(slot // num_dp, c, lax.rem(slot, num_dp)),
            device_id_type=MESH,
        ).start()

    gathered[my_slot] = item_emb
    others_b = pl.ds(0, slots - 1)
    pltpu.make_async_copy(gathered.at[others_b], gathered.at[others_b], recv_b).wait()
    for s in range(slots):
        items_flat[s * per_block : (s + 1) * per_block, :] = gathered[s]
    item_hi, item_lo = split2(items_flat[...])
    count = slots * per_block
    column = min(users, 256)

    @pl.loop(0, users // column)
    def _(u):
        rows = pl.ds(pl.multiple_of(u * column, column), column)
        uh, ul = user_hi[rows, :], user_lo[rows, :]

        def cross(a, b):
            return lax.dot_general(a, b, (((1,), (1,)), ((), ())), preferred_element_type=F32)

        scores = cross(item_lo, uh) + cross(item_hi, ul) + cross(item_hi, uh)
        line = lax.broadcasted_iota(jnp.int32, (count, 1), 0)
        slot = line // per_block
        ids = ((slot // num_dp * num_cand + c) * num_dp + slot % num_dp) * per_block + line % per_block
        sums_here[0:1, rows] = jnp.sum(jnp.exp(scores), axis=0, keepdims=True)
        sums_here[1:2, rows] = jnp.sum(
            jnp.where(ids == positives[:, rows], scores, jnp.float32(0.0)), axis=0, keepdims=True
        )

    @pl.loop(1, num_cand)
    def _(j):
        peer = lax.rem(c + j, num_cand)
        pltpu.make_async_remote_copy(
            src_ref=sums_here,
            dst_ref=sums_all.at[c],
            send_sem=send_c,
            recv_sem=recv_c,
            device_id=(t, peer, d),
            device_id_type=MESH,
        ).start()

    sums_all[c] = sums_here[...]
    others_c = pl.ds(0, num_cand - 1)
    pltpu.make_async_copy(sums_all.at[others_c], sums_all.at[others_c], recv_c).wait()
    both = sums_all[0]
    for s in range(1, num_cand):
        both = both + sums_all[s]
    loss_out[...] = jnp.log(both[0:1, :]) - both[1:2, :]

    pltpu.make_async_copy(pooled.at[others], pooled.at[others], send_a).wait()
    pltpu.make_async_copy(gathered.at[others_b], gathered.at[others_b], send_b).wait()
    pltpu.make_async_copy(sums_all.at[others_c], sums_all.at[others_c], send_c).wait()


def body(
    tables, bag_ids, bag_lengths, item_weight, user_features, user_w1, user_w2, positive_items
):
    sizes = tuple(lax.axis_size(n) for n in ("tab", "cand", "dp"))
    total = math.prod(sizes)
    slots = sizes[0] * sizes[2]
    table = tables[0]
    rows, width = table.shape
    items, length = bag_ids.shape[1:]
    per_block = items // total
    users = user_features.shape[0]
    embed = user_w2.shape[1]
    local = bag_ids[0].T - lax.axis_index("tab") * rows
    valid = lax.broadcasted_iota(jnp.int32, local.shape, 0) < bag_lengths
    keeping = (local >= 0) & (local < rows) & valid
    ids = jnp.where(keeping, local, rows)
    inverse = 1.0 / bag_lengths[0].astype(F32)
    tile = 128
    chunks = users // tile // 2
    vmem = pl.BlockSpec(memory_space=pltpu.VMEM)
    smem = pl.BlockSpec(memory_space=pltpu.SMEM)
    anywhere = pl.BlockSpec(memory_space=pl.ANY)
    item_emb, loss = pl.pallas_call(
        functools.partial(main_kernel, sizes, length),
        out_shape=(
            jax.ShapeDtypeStruct((per_block, embed), F32),
            jax.ShapeDtypeStruct((1, users), F32),
        ),
        in_specs=[smem] * (length + 1) + [anywhere] * 5 + [vmem],
        out_specs=(vmem, vmem),
        scratch_shapes=[
            pltpu.VMEM((rows, width), BF16),
            pltpu.VMEM((rows + 8, width), F32),
            pltpu.VMEM(item_weight.shape, BF16),
            pltpu.VMEM(user_features.shape, BF16),
            pltpu.VMEM(user_w1.shape, BF16),
            pltpu.VMEM(user_w2.shape, BF16),
            pltpu.VMEM((total, per_block, width), F32),
            pltpu.VMEM((total, per_block, width), F32),
            pltpu.VMEM((per_block, item_weight.shape[0]), F32),
            pltpu.VMEM((tile, embed), F32),
            pltpu.VMEM((users, embed), BF16),
            pltpu.VMEM((users, embed), BF16),
            pltpu.VMEM((slots, per_block, embed), F32),
            pltpu.VMEM((slots * per_block, embed), F32),
            pltpu.VMEM((2, users), F32),
            pltpu.VMEM((sizes[1], 2, users), F32),
            pltpu.SemaphoreType.DMA((4,)),
            pltpu.SemaphoreType.DMA((chunks,)),
        ]
        + [pltpu.SemaphoreType.DMA] * 6,
        compiler_params=pltpu.CompilerParams(
            collective_id=0, has_side_effects=True, vmem_limit_bytes=VMEM_LIMIT
        ),
        name="step",
    )(
        *[ids[p] for p in range(length)],
        inverse,
        table,
        item_weight,
        user_features,
        user_w1,
        user_w2,
        positive_items[None, :],
    )
    return (item_emb, loss[0])


def solution(mesh):
    placed = (
        P(("cand", "dp"), "tab", None),
        P(("cand", "dp"), None, None),
        P(("cand", "dp"), None),
        P(),
        P(("tab", "dp"), None),
        P(),
        P(),
        P(("tab", "dp")),
    )
    return jax.shard_map(
        body,
        mesh=mesh,
        in_specs=placed,
        out_specs=(P(("tab", "cand", "dp"), None), P(("tab", "dp"))),
        check_vma=False,
    )
```

profile of v0, /device:TPU:0, one launch (start us, length us, event | category | flops | bytes accessed | tf_op | source)
XLA Modules:
  0.0 59.1 jit_solution(2216253437816136074)
XLA Ops:
  0.6 0.9 %bitcast_select_fusion = s32[16,1024]{1,0:T(8,128)S(1)} fusion(s32[1,1024,16]{1,2,0:T(8,128)} %param.9, s32[1024]{0:T(1024)} %bitcast.49, s32[]{:T(128)S(6)} %mul.3), kind=kLoop, calls=%fused_computation | loop fusion | flops 114688 | bytes 135172 | tf_op jit(solution)/shard_map/jit(_where)/select_n | solution.py:306
  1.5 0.7 %fusion.2 = (s32[1,1024]{1,0:T(1,128)}, s32[1,1024]{1,0:T(1,128)}, s32[1,1024]{1,0:T(1,128)}, s32[1,1024]{1,0:T(1,128)}, s32[1,1024]{1,0:T(1,128)}, /*index=5*/s...) fusion(s32[16,1024]{1,0:T(8,128)S(1)} %bitcast_select_fusion), kind=kLoop, calls=%fused_computation.7 | loop fusion | bytes 131072 | tf_op jit(solution)/shard_map/slice | solution.py:347
  2.2 1.3 %convert_divide_fusion.refs_16_ = f32[1024]{0:T(1024)} fusion(s32[1024]{0:T(1024)} %bitcast.50), kind=kLoop, calls=%fused_computation.6 | loop fusion | flops 2048 | bytes 8192 | tf_op jit(solution)/shard_map/div | solution.py:307
  3.5 53.0 %step.1 = (f32[32,256]{1,0:T(8,128)}, f32[1,2048]{1,0:T(1,128)}) custom-call(s32[1024]{0:T(1024)} %bitcast.48, s32[1024]{0:T(1024)} %bitcast.47, s32[1024]{0:T(1024)} %bitcast.46, s32[1024]{0:T(1024)} %bitcast.45, s32[1024]{0:T(1024)} %bitcast.44, s32[1024]{0:T(1024)} %bitcast.43, s32[1024]{0:T(1024)} %bitcast.42, s32[1024]{0:T(1024)} %bitcast.41, ...), custom_call_target="tpu_custom_call" | custom-call | tf_op jit(solution)/shard_map/step/pallas_call | solution.py:313
  56.5 1.4 %copy.12 = f32[32,256]{1,0:T(8,128)} copy(f32[32,256]{1,0:T(8,128)} %get-tuple-element.24) | data formatting | bytes 65536
  57.8 1.3 %copy.13 = f32[2048]{0:T(1024)} copy(f32[2048]{0:T(1024)} %bitcast.51) | data formatting | bytes 16384
where the time goes:
time: 59.5 us; the launch traced here: 59.1 us
  Pallas kernels  53 us (89%)
  local copies, waits for them, and re-layouts  3.34 us (6%)
  other arithmetic  2.15 us (4%)
  between operations  0.65 us (1%)
    pallas_call x1, Pallas kernels, body(): pl.pallas_call(functools.partial(main_kernel, sizes, length), out_shape=(...  53 us
    unnamed x2, local copies, waits for them, and re-layouts  2.67 us
    div x1, other arithmetic, body(): inverse = 1.0 / bag_lengths[0].astype(F32)  1.28 us

commit v1 on v0

v1 whole, which is shorter than its diff:
```python
import functools
import math

import jax
import jax.numpy as jnp
from jax import lax
from jax.experimental import pallas as pl
from jax.experimental.pallas import tpu as pltpu
from jax.sharding import PartitionSpec as P

epsilon = 1e-06
logit_scale = 20.0
MESH = pl.DeviceIdType.MESH
F32 = jnp.float32
BF16 = jnp.bfloat16
VMEM_LIMIT = 60 * 1024 * 1024
LANES = 128
SUBLANES = 8
ZERO_ROWS = 32


def split2(x):
    hi = x.astype(BF16)
    return hi, (x - hi.astype(F32)).astype(BF16)


def unit_rows(vectors):
    return vectors * lax.rsqrt(jnp.mean(vectors * vectors, axis=-1, keepdims=True) + epsilon)


def dot(a, b):
    return jnp.dot(a, b, preferred_element_type=F32)


def run_step(
    sizes,
    ids_in,
    lengths_in,
    table,
    weight_in,
    features_in,
    w1_in,
    w2_in,
    positives_in,
    emb_out,
    loss_out,
    ids_raw,
    lengths,
    index_rows,
    inverse,
    narrow,
    wide,
    weight,
    features,
    w1,
    w2,
    positives,
    pooled,
    arrived,
    joined,
    emb,
    user_hi,
    user_lo,
    gathered,
    items_flat,
    sums_here,
    sums_all,
    loss,
    load_sems,
    table_sems,
    index_sems,
    out_sems,
    send_a,
    recv_a,
    send_b,
    recv_b,
    send_c,
    recv_c,
    *index,
):
    num_tab, num_cand, num_dp = sizes
    total = num_tab * num_cand * num_dp
    groups = num_cand * num_dp
    slots = num_tab * num_dp
    t, c, d = (lax.axis_index(n) for n in ("tab", "cand", "dp"))
    me = (t * num_cand + c) * num_dp + d
    my_slot = t * num_dp + d
    per_block, width = pooled.shape[1:]
    items = total * per_block
    length = ids_raw.shape[0]
    rows, _ = table.shape
    users = features.shape[0]
    hidden = w1.shape[1]
    embed = w2.shape[1]
    chunks = table_sems.shape[0]
    chunk = rows // chunks
    held = narrow.shape[0]
    blocks_step = max(1, 32 // per_block)
    steps = total // blocks_step
    items_step = items // steps
    columns = items // LANES

    def place(index):
        return (index // groups, index // num_dp % num_cand, index % num_dp)

    barrier = pltpu.get_barrier_semaphore()

    loads = [
        pltpu.make_async_copy(a, b, load_sems.at[i])
        for i, (a, b) in enumerate(
            (
                (ids_in, ids_raw),
                (lengths_in, lengths),
                (w1_in, w1),
                (w2_in, w2),
                (features_in, features),
                (weight_in, weight),
                (positives_in, positives),
            )
        )
    ]

    def chunk_copy(n):
        part = pl.ds(pl.multiple_of(n * chunk, chunk), chunk)
        return pltpu.make_async_copy(table.at[part], narrow.at[lax.rem(n, held)], table_sems.at[n])

    for load in loads[:2]:
        load.start()
    for n in range(min(chunks, held)):
        chunk_copy(n).start()
    for load in loads[2:]:
        load.start()

    @pl.loop(1, total)
    def _(j):
        peer = lax.rem(me + j, total)
        pl.semaphore_signal(barrier, inc=1, device_id=place(peer), device_id_type=MESH)

    wide[pl.ds(rows, ZERO_ROWS), :] = jnp.zeros((ZERO_ROWS, width), F32)
    for load in loads[:2]:
        load.wait()
    first_row = t * rows
    spread = lax.broadcasted_iota(jnp.int32, (SUBLANES, LANES), 1) % 2 * (ZERO_ROWS // 2)
    line = lax.broadcasted_iota(jnp.int32, (SUBLANES, LANES), 0)
    for b in range(columns):
        lanes = slice(b * LANES, (b + 1) * LANES)
        count = lengths[:, lanes]
        for p in range(0, length, SUBLANES):
            local = ids_raw[p : p + SUBLANES, lanes] - first_row
            position = line + p
            keeping = (local >= 0) & (local < rows) & (position < count)
            spare = rows + position % (ZERO_ROWS // 2) + spread
            index_rows[p : p + SUBLANES, lanes] = jnp.where(keeping, local, spare)
    index_copies = [
        pltpu.make_async_copy(index_rows.at[p], index[p], index_sems.at[p]) for p in range(length)
    ]
    for copy in index_copies:
        copy.start()
    for b in range(columns):
        lanes = slice(b * LANES, (b + 1) * LANES)
        scale = 1.0 / lengths[:, lanes].astype(F32)
        inverse[lanes, :] = jnp.broadcast_to(scale, (LANES, LANES)).T

    @pl.loop(0, chunks)
    def _(n):
        chunk_copy(n).wait()
        part = pl.ds(pl.multiple_of(n * chunk, chunk), chunk)
        wide[part, :] = narrow[lax.rem(n, held)].astype(F32)
        if held < chunks:

            @pl.when(n + held < chunks)
            def _():
                chunk_copy(n + held).start()

    for copy in index_copies:
        copy.wait()
    pl.semaphore_wait(barrier, total - 1)

    def send(dest):
        pltpu.make_async_remote_copy(
            src_ref=pooled.at[dest],
            dst_ref=arrived.at[me],
            send_sem=send_a,
            recv_sem=recv_a,
            device_id=place(dest),
            device_id_type=MESH,
        ).start()

    def group_at(s):
        if blocks_step > 1 or num_cand != 4:
            return lax.rem(me // blocks_step + 1 + s, steps)
        turn = s // slots
        plane = jnp.where(
            turn == 0,
            (c + 2) % 4,
            jnp.where(turn == 1, 3 - c, jnp.where(turn == 2, c + 1 - c % 2 * 2, c)),
        )
        slot = lax.rem(my_slot + 1 + s, slots)
        return (slot // num_dp * num_cand + plane) * num_dp + slot % num_dp

    @pl.loop(0, steps)
    def _(s):
        @pl.when(s > 0)
        def _():
            before = group_at(s - 1)
            for i in range(blocks_step):
                send(before * blocks_step + i)

        group = group_at(s)
        first = group * items_step
        for k in range(items_step):
            terms = [wide[pl.ds(of_place[first + k], 1), :] for of_place in index]
            while len(terms) > 1:
                terms = [a + b for a, b in zip(terms[::2], terms[1::2])] + (
                    [terms[-1]] if len(terms) % 2 else []
                )
            row = terms[0] * inverse[pl.ds(first + k, 1), :]
            pooled[group * blocks_step + k // per_block, pl.ds(k % per_block, 1), :] = row

    last = group_at(steps - 1)
    for i in range(blocks_step):
        dest = last * blocks_step + i
        if blocks_step > 1:

            @pl.when(dest != me)
            def _():
                send(dest)

    for load in loads[2:]:
        load.wait()
    tile = min(users, TILE)
    part_width = min(hidden, 256)

    @pl.loop(0, users // tile)
    def _(n):
        user_rows = pl.ds(pl.multiple_of(n * tile, tile), tile)
        x = features[user_rows, :]
        pre = None
        for h in range(0, hidden, part_width):
            z = dot(x, w1[:, h : h + part_width])
            z = z * (0.5 * lax.erf(z * math.sqrt(0.5)) + 0.5)
            term = dot(z.astype(BF16), w2[h : h + part_width, :])
            pre = term if pre is None else pre + term
        hi, lo = split2(unit_rows(pre) * (logit_scale / embed))
        user_hi[user_rows, :] = hi
        user_lo[user_rows, :] = lo

    arrived[me] = pooled[me]
    others = pl.ds(0, total - 1)
    pltpu.make_async_copy(arrived.at[others], arrived.at[others], recv_a).wait()
    for f in range(groups):
        block = arrived[f]
        for s in range(1, num_tab):
            block = block + arrived[s * groups + f]
        joined[:, f * width : (f + 1) * width] = block
    hi, lo = split2(joined[...])
    both = dot(jnp.concatenate([hi, lo], axis=0), weight[...])
    item_emb = unit_rows(both[:per_block] + both[per_block:])
    emb[...] = item_emb

    @pl.loop(1, slots)
    def _(j):
        slot = lax.rem(my_slot + j, slots)
        pltpu.make_async_remote_copy(
            src_ref=emb,
            dst_ref=gathered.at[my_slot],
            send_sem=send_b,
            recv_sem=recv_b,
            device_id=(slot // num_dp, c, lax.rem(slot, num_dp)),
            device_id_type=MESH,
        ).start()

    emb_copy = pltpu.make_async_copy(emb, emb_out, out_sems.at[0])
    emb_copy.start()
    gathered[my_slot] = item_emb
    others_b = pl.ds(0, slots - 1)
    pltpu.make_async_copy(gathered.at[others_b], gathered.at[others_b], recv_b).wait()
    for s in range(slots):
        items_flat[s * per_block : (s + 1) * per_block, :] = gathered[s]
    item_hi, item_lo = split2(items_flat[...])
    count = slots * per_block
    column = min(users, 256)

    @pl.loop(0, users // column)
    def _(u):
        rows = pl.ds(pl.multiple_of(u * column, column), column)
        uh, ul = user_hi[rows, :], user_lo[rows, :]

        def cross(a, b):
            return lax.dot_general(a, b, (((1,), (1,)), ((), ())), preferred_element_type=F32)

        scores = cross(item_lo, uh) + cross(item_hi, ul) + cross(item_hi, uh)
        line = lax.broadcasted_iota(jnp.int32, (count, 1), 0)
        slot = line // per_block
        ids = ((slot // num_dp * num_cand + c) * num_dp + slot % num_dp) * per_block + line % per_block
        sums_here[0:1, rows] = jnp.sum(jnp.exp(scores), axis=0, keepdims=True)
        sums_here[1:2, rows] = jnp.sum(
            jnp.where(ids == positives[:, rows], scores, jnp.float32(0.0)), axis=0, keepdims=True
        )

    @pl.loop(1, num_cand)
    def _(j):
        peer = lax.rem(c + j, num_cand)
        pltpu.make_async_remote_copy(
            src_ref=sums_here,
            dst_ref=sums_all.at[c],
            send_sem=send_c,
            recv_sem=recv_c,
            device_id=(t, peer, d),
            device_id_type=MESH,
        ).start()

    sums_all[c] = sums_here[...]
    others_c = pl.ds(0, num_cand - 1)
    pltpu.make_async_copy(sums_all.at[others_c], sums_all.at[others_c], recv_c).wait()
    both = sums_all[0]
    for s in range(1, num_cand):
        both = both + sums_all[s]
    loss[...] = jnp.log(both[0:1, :]) - both[1:2, :]
    loss_copy = pltpu.make_async_copy(loss, loss_out, out_sems.at[1])
    loss_copy.start()

    pltpu.make_async_copy(pooled.at[others], pooled.at[others], send_a).wait()
    pltpu.make_async_copy(gathered.at[others_b], gathered.at[others_b], send_b).wait()
    pltpu.make_async_copy(sums_all.at[others_c], sums_all.at[others_c], send_c).wait()
    emb_copy.wait()
    loss_copy.wait()


TILE = 256


def body(
    tables, bag_ids, bag_lengths, item_weight, user_features, user_w1, user_w2, positive_items
):
    sizes = tuple(lax.axis_size(n) for n in ("tab", "cand", "dp"))
    total = math.prod(sizes)
    slots = sizes[0] * sizes[2]
    table = tables[0]
    rows, width = table.shape
    items, length = bag_ids.shape[1:]
    per_block = items // total
    users = user_features.shape[0]
    embed = user_w2.shape[1]
    chunk = min(rows, 4096)
    chunks = rows // chunk
    held = min(chunks, 8)
    anywhere = pl.BlockSpec(memory_space=pl.ANY)
    item_emb, loss = pl.pallas_call(
        functools.partial(run_step, sizes),
        out_shape=(
            jax.ShapeDtypeStruct((per_block, embed), F32),
            jax.ShapeDtypeStruct((1, users), F32),
        ),
        in_specs=[anywhere] * 8,
        out_specs=(anywhere, anywhere),
        scratch_shapes=[
            pltpu.VMEM((length, items), jnp.int32),
            pltpu.VMEM((1, items), jnp.int32),
            pltpu.VMEM((length, items), jnp.int32),
            pltpu.VMEM((items, LANES), F32),
            pltpu.VMEM((held, chunk, width), BF16),
            pltpu.VMEM((rows + ZERO_ROWS, width), F32),
            pltpu.VMEM(item_weight.shape, BF16),
            pltpu.VMEM(user_features.shape, BF16),
            pltpu.VMEM(user_w1.shape, BF16),
            pltpu.VMEM(user_w2.shape, BF16),
            pltpu.VMEM((1, users), jnp.int32),
            pltpu.VMEM((total, per_block, width), F32),
            pltpu.VMEM((total, per_block, width), F32),
            pltpu.VMEM((per_block, item_weight.shape[0]), F32),
            pltpu.VMEM((per_block, embed), F32),
            pltpu.VMEM((users, embed), BF16),
            pltpu.VMEM((users, embed), BF16),
            pltpu.VMEM((slots, per_block, embed), F32),
            pltpu.VMEM((slots * per_block, embed), F32),
            pltpu.VMEM((2, users), F32),
            pltpu.VMEM((sizes[1], 2, users), F32),
            pltpu.VMEM((1, users), F32),
            pltpu.SemaphoreType.DMA((7,)),
            pltpu.SemaphoreType.DMA((chunks,)),
            pltpu.SemaphoreType.DMA((length,)),
            pltpu.SemaphoreType.DMA((2,)),
        ]
        + [pltpu.SemaphoreType.DMA] * 6
        + [pltpu.SMEM((items,), jnp.int32)] * length,
        compiler_params=pltpu.CompilerParams(
            collective_id=0, has_side_effects=True, vmem_limit_bytes=VMEM_LIMIT
        ),
        name="step",
    )(
        bag_ids[0].T,
        bag_lengths,
        table,
        item_weight,
        user_features,
        user_w1,
        user_w2,
        positive_items[None, :],
    )
    return (item_emb, loss[0])


def solution(mesh):
    placed = (
        P(("cand", "dp"), "tab", None),
        P(("cand", "dp"), None, None),
        P(("cand", "dp"), None),
        P(),
        P(("tab", "dp"), None),
        P(),
        P(),
        P(("tab", "dp")),
    )
    return jax.shard_map(
        body,
        mesh=mesh,
        in_specs=placed,
        out_specs=(P(("tab", "cand", "dp"), None), P(("tab", "dp"))),
        check_vma=False,
    )
```

time: 59.5 us -> 42.5 us (0.71)
  Pallas kernels: 53 us -> 39 us
  other arithmetic: 2.15 us -> 0 us
  local copies, waits for them, and re-layouts: 3.34 us -> 2.67 us
    pallas_call x1, Pallas kernels: 53 us -> 39 us  [body(): pl.pallas_call(functools.partial(run_step, sizes), out_shape=(jax.ShapeDt...]
    div x1 -> x0, other arithmetic: 1.28 us -> none  [body(): inverse = 1.0 / bag_lengths[0].astype(F32)]
    select_n x1 -> x0, other arithmetic: 0.86 us -> none  [body(): ids = jnp.where(keeping, local, rows)]
    slice x1 -> x0, local copies, waits for them, and re-layouts: 0.67 us -> none  [body(): ids[p]]
where the time goes in v1:
time: 42.5 us; the launch traced here: 42.3 us
  Pallas kernels  39 us (92%)
  local copies, waits for them, and re-layouts  2.67 us (6%)
  between operations  0.64 us (2%)
    pallas_call x1, Pallas kernels, body(): pl.pallas_call(functools.partial(run_step, sizes), out_shape=(jax.ShapeDt...  39 us
    unnamed x2, local copies, waits for them, and re-layouts  2.67 us

profile of v1, /device:TPU:0, one launch (start us, length us, event | category | flops | bytes accessed | tf_op | source)
XLA Modules:
  0.0 42.3 jit_solution(10600431790425436424)
XLA Ops:
  0.6 39.0 %step.1 = (f32[32,256]{1,0:T(8,128)}, f32[1,2048]{1,0:T(1,128)}) custom-call(s32[16,1024]{1,0:T(8,128)} %bitcast.7, s32[1,1024]{1,0:T(1,128)} %lengths_in.1, bf16[32768,128]{1,0:T(8,128)(2,1)} %bitcast.6, bf16[2048,256]{1,0:T(8,128)(2,1)} %weight_in.1, bf16[2048,512]{1,0:T(8,128)(2,1)} %features_in.1, bf16[512,1024]{1,0:T(8,128)(2,1)} %w1_in.1, ...), custom_call_target="tpu_custom_call" | custom-call | tf_op jit(solution)/shard_map/step/pallas_call | solution.py:349
  39.6 1.4 %copy.12 = f32[32,256]{1,0:T(8,128)} copy(f32[32,256]{1,0:T(8,128)} %get-tuple-element.8) | data formatting | bytes 65536
  41.0 1.3 %copy.13 = f32[2048]{0:T(1024)} copy(f32[2048]{0:T(1024)} %bitcast.8) | data formatting | bytes 16384

commit v2 on v1

--- a/solution.py
+++ b/solution.py
@@ -76,6 +76,7 @@
     recv_b,
     send_c,
     recv_c,
+    ready,
     *index,
 ):
     num_tab, num_cand, num_dp = sizes
@@ -124,18 +125,24 @@
         part = pl.ds(pl.multiple_of(n * chunk, chunk), chunk)
         return pltpu.make_async_copy(table.at[part], narrow.at[lax.rem(n, held)], table_sems.at[n])
 
+    def in_plane(slot):
+        return (slot // num_dp, c, slot % num_dp)
+
     for load in loads[:2]:
         load.start()
+
+    @pl.loop(1, num_cand)
+    def _(j):
+        peer = (t, lax.rem(c + j, num_cand), d)
+        pl.semaphore_signal(barrier, inc=1, device_id=peer, device_id_type=MESH)
+
+    @pl.loop(1, slots)
+    def _(j):
+        peer = in_plane(lax.rem(my_slot + j, slots))
+        pl.semaphore_signal(barrier, inc=1, device_id=peer, device_id_type=MESH)
+
     for n in range(min(chunks, held)):
         chunk_copy(n).start()
-    for load in loads[2:]:
-        load.start()
-
-    @pl.loop(1, total)
-    def _(j):
-        peer = lax.rem(me + j, total)
-        pl.semaphore_signal(barrier, inc=1, device_id=place(peer), device_id_type=MESH)
-
     wide[pl.ds(rows, ZERO_ROWS), :] = jnp.zeros((ZERO_ROWS, width), F32)
     for load in loads[:2]:
         load.wait()
@@ -161,6 +168,13 @@
         scale = 1.0 / lengths[:, lanes].astype(F32)
         inverse[lanes, :] = jnp.broadcast_to(scale, (LANES, LANES)).T
 
+    pl.semaphore_wait(barrier, num_cand - 1 + slots - 1)
+
+    @pl.loop(1, slots)
+    def _(j):
+        peer = in_plane(lax.rem(my_slot + j, slots))
+        pl.semaphore_signal(ready, inc=1, device_id=peer, device_id_type=MESH)
+
     @pl.loop(0, chunks)
     def _(n):
         chunk_copy(n).wait()
@@ -172,9 +186,10 @@
             def _():
                 chunk_copy(n + held).start()
 
+    for load in loads[2:]:
+        load.start()
     for copy in index_copies:
         copy.wait()
-    pl.semaphore_wait(barrier, total - 1)
 
     def send(dest):
         pltpu.make_async_remote_copy(
@@ -200,6 +215,10 @@
 
     @pl.loop(0, steps)
     def _(s):
+        @pl.when(s == 1)
+        def _():
+            pl.semaphore_wait(ready, slots - 1)
+
         @pl.when(s > 0)
         def _():
             before = group_at(s - 1)
@@ -231,8 +250,7 @@
     tile = min(users, TILE)
     part_width = min(hidden, 256)
 
-    @pl.loop(0, users // tile)
-    def _(n):
+    def tower(n):
         user_rows = pl.ds(pl.multiple_of(n * tile, tile), tile)
         x = features[user_rows, :]
         pre = None
@@ -244,6 +262,10 @@
         hi, lo = split2(unit_rows(pre) * (logit_scale / embed))
         user_hi[user_rows, :] = hi
         user_lo[user_rows, :] = lo
+
+    tiles = users // tile
+    early = tiles * EARLY // 8
+    pl.loop(0, early)(tower)
 
     arrived[me] = pooled[me]
     others = pl.ds(0, total - 1)
@@ -266,13 +288,14 @@
             dst_ref=gathered.at[my_slot],
             send_sem=send_b,
             recv_sem=recv_b,
-            device_id=(slot // num_dp, c, lax.rem(slot, num_dp)),
+            device_id=in_plane(slot),
             device_id_type=MESH,
         ).start()
 
     emb_copy = pltpu.make_async_copy(emb, emb_out, out_sems.at[0])
     emb_copy.start()
     gathered[my_slot] = item_emb
+    pl.loop(early, tiles)(tower)
     others_b = pl.ds(0, slots - 1)
     pltpu.make_async_copy(gathered.at[others_b], gathered.at[others_b], recv_b).wait()
     for s in range(slots):
@@ -328,6 +351,7 @@
 
 
 TILE = 256
+EARLY = 2
 
 
 def body(
@@ -383,6 +407,7 @@
             pltpu.SemaphoreType.DMA((2,)),
         ]
         + [pltpu.SemaphoreType.DMA] * 6
+        + [pltpu.SemaphoreType.REGULAR]
         + [pltpu.SMEM((items,), jnp.int32)] * length,
         compiler_params=pltpu.CompilerParams(
             collective_id=0, has_side_effects=True, vmem_limit_bytes=VMEM_LIMIT

time: 42.5 us -> 38.1 us (0.90)
  Pallas kernels: 39 us -> 34.6 us
    pallas_call x1, Pallas kernels: 39 us -> 34.6 us  [body(): pl.pallas_call(functools.partial(run_step, sizes), out_shape=(jax.ShapeDt...]
where the time goes in v2:
time: 38.1 us; the launch traced here: 37.9 us
  Pallas kernels  34.6 us (91%)
  local copies, waits for them, and re-layouts  2.67 us (7%)
  between operations  0.64 us (2%)
    pallas_call x1, Pallas kernels, body(): pl.pallas_call(functools.partial(run_step, sizes), out_shape=(jax.ShapeDt...  34.6 us
    unnamed x2, local copies, waits for them, and re-layouts  2.67 us

profile of v2, /device:TPU:0, one launch (start us, length us, event | category | flops | bytes accessed | tf_op | source)
XLA Modules:
  0.0 37.9 jit_solution(7938546958925896876)
XLA Ops:
  0.6 34.6 %step.1 = (f32[32,256]{1,0:T(8,128)}, f32[1,2048]{1,0:T(1,128)}) custom-call(s32[16,1024]{1,0:T(8,128)} %bitcast.7, s32[1,1024]{1,0:T(1,128)} %lengths_in.1, bf16[32768,128]{1,0:T(8,128)(2,1)} %bitcast.6, bf16[2048,256]{1,0:T(8,128)(2,1)} %weight_in.1, bf16[2048,512]{1,0:T(8,128)(2,1)} %features_in.1, bf16[512,1024]{1,0:T(8,128)(2,1)} %w1_in.1, ...), custom_call_target="tpu_custom_call" | custom-call | tf_op jit(solution)/shard_map/step/pallas_call | solution.py:373
  35.2 1.4 %copy.12 = f32[32,256]{1,0:T(8,128)} copy(f32[32,256]{1,0:T(8,128)} %get-tuple-element.8) | data formatting | bytes 65536
  36.6 1.3 %copy.13 = f32[2048]{0:T(1024)} copy(f32[2048]{0:T(1024)} %bitcast.8) | data formatting | bytes 16384

commit v3 on v2

--- a/solution.py
+++ b/solution.py
@@ -58,18 +58,15 @@
     pooled,
     arrived,
     joined,
-    emb,
     user_hi,
     user_lo,
     gathered,
     items_flat,
     sums_here,
     sums_all,
-    loss,
     load_sems,
     table_sems,
     index_sems,
-    out_sems,
     send_a,
     recv_a,
     send_b,
@@ -256,10 +253,10 @@
         pre = None
         for h in range(0, hidden, part_width):
             z = dot(x, w1[:, h : h + part_width])
-            z = z * (0.5 * lax.erf(z * math.sqrt(0.5)) + 0.5)
+            z = z * lax.erf(z * math.sqrt(0.5)) + z
             term = dot(z.astype(BF16), w2[h : h + part_width, :])
             pre = term if pre is None else pre + term
-        hi, lo = split2(unit_rows(pre) * (logit_scale / embed))
+        hi, lo = split2(unit_rows(pre * 0.5) * (logit_scale / embed * math.log2(math.e)))
         user_hi[user_rows, :] = hi
         user_lo[user_rows, :] = lo
 
@@ -278,13 +275,13 @@
     hi, lo = split2(joined[...])
     both = dot(jnp.concatenate([hi, lo], axis=0), weight[...])
     item_emb = unit_rows(both[:per_block] + both[per_block:])
-    emb[...] = item_emb
+    emb_out[...] = item_emb
 
     @pl.loop(1, slots)
     def _(j):
         slot = lax.rem(my_slot + j, slots)
         pltpu.make_async_remote_copy(
-            src_ref=emb,
+            src_ref=emb_out,
             dst_ref=gathered.at[my_slot],
             send_sem=send_b,
             recv_sem=recv_b,
@@ -292,8 +289,6 @@
             device_id_type=MESH,
         ).start()
 
-    emb_copy = pltpu.make_async_copy(emb, emb_out, out_sems.at[0])
-    emb_copy.start()
     gathered[my_slot] = item_emb
     pl.loop(early, tiles)(tower)
     others_b = pl.ds(0, slots - 1)
@@ -302,7 +297,11 @@
         items_flat[s * per_block : (s + 1) * per_block, :] = gathered[s]
     item_hi, item_lo = split2(items_flat[...])
     count = slots * per_block
-    column = min(users, 256)
+    column = min(users, COLUMN)
+
+    line = lax.broadcasted_iota(jnp.int32, (count, 1), 0)
+    slot = line // per_block
+    ids = ((slot // num_dp * num_cand + c) * num_dp + slot % num_dp) * per_block + line % per_block
 
     @pl.loop(0, users // column)
     def _(u):
@@ -313,10 +312,7 @@
             return lax.dot_general(a, b, (((1,), (1,)), ((), ())), preferred_element_type=F32)
 
         scores = cross(item_lo, uh) + cross(item_hi, ul) + cross(item_hi, uh)
-        line = lax.broadcasted_iota(jnp.int32, (count, 1), 0)
-        slot = line // per_block
-        ids = ((slot // num_dp * num_cand + c) * num_dp + slot % num_dp) * per_block + line % per_block
-        sums_here[0:1, rows] = jnp.sum(jnp.exp(scores), axis=0, keepdims=True)
+        sums_here[0:1, rows] = jnp.sum(jnp.exp2(scores), axis=0, keepdims=True)
         sums_here[1:2, rows] = jnp.sum(
             jnp.where(ids == positives[:, rows], scores, jnp.float32(0.0)), axis=0, keepdims=True
         )
@@ -339,19 +335,16 @@
     both = sums_all[0]
     for s in range(1, num_cand):
         both = both + sums_all[s]
-    loss[...] = jnp.log(both[0:1, :]) - both[1:2, :]
-    loss_copy = pltpu.make_async_copy(loss, loss_out, out_sems.at[1])
-    loss_copy.start()
+    loss_out[...] = jnp.log(both[0:1, :]) - both[1:2, :] * math.log(2.0)
 
     pltpu.make_async_copy(pooled.at[others], pooled.at[others], send_a).wait()
     pltpu.make_async_copy(gathered.at[others_b], gathered.at[others_b], send_b).wait()
     pltpu.make_async_copy(sums_all.at[others_c], sums_all.at[others_c], send_c).wait()
-    emb_copy.wait()
-    loss_copy.wait()
-
-
-TILE = 256
+
+
+TILE = 512
 EARLY = 2
+COLUMN = 512
 
 
 def body(
@@ -369,15 +362,16 @@
     chunk = min(rows, 4096)
     chunks = rows // chunk
     held = min(chunks, 8)
-    anywhere = pl.BlockSpec(memory_space=pl.ANY)
+    far = pl.BlockSpec(memory_space=pltpu.HBM)
+    near = pl.BlockSpec(memory_space=pltpu.VMEM)
     item_emb, loss = pl.pallas_call(
         functools.partial(run_step, sizes),
         out_shape=(
-            jax.ShapeDtypeStruct((per_block, embed), F32),
-            jax.ShapeDtypeStruct((1, users), F32),
+            pltpu.VMEM((per_block, embed), F32),
+            pltpu.VMEM((1, users), F32),
         ),
-        in_specs=[anywhere] * 8,
-        out_specs=(anywhere, anywhere),
+        in_specs=[far] * 8,
+        out_specs=(near, near),
         scratch_shapes=[
             pltpu.VMEM((length, items), jnp.int32),
             pltpu.VMEM((1, items), jnp.int32),
@@ -393,18 +387,15 @@
             pltpu.VMEM((total, per_block, width), F32),
             pltpu.VMEM((total, per_block, width), F32),
             pltpu.VMEM((per_block, item_weight.shape[0]), F32),
-            pltpu.VMEM((per_block, embed), F32),
             pltpu.VMEM((users, embed), BF16),
             pltpu.VMEM((users, embed), BF16),
             pltpu.VMEM((slots, per_block, embed), F32),
             pltpu.VMEM((slots * per_block, embed), F32),
             pltpu.VMEM((2, users), F32),
             pltpu.VMEM((sizes[1], 2, users), F32),
-            pltpu.VMEM((1, users), F32),
             pltpu.SemaphoreType.DMA((7,)),
             pltpu.SemaphoreType.DMA((chunks,)),
             pltpu.SemaphoreType.DMA((length,)),
-            pltpu.SemaphoreType.DMA((2,)),
         ]
         + [pltpu.SemaphoreType.DMA] * 6
         + [pltpu.SemaphoreType.REGULAR]

time: 38.1 us -> 35 us (0.919)
  Pallas kernels: 34.6 us -> 33 us
  local copies, waits for them, and re-layouts: 2.67 us -> 1.22 us
    pallas_call x1, Pallas kernels: 34.6 us -> 33 us  [body(): pl.pallas_call(functools.partial(run_step, sizes), out_shape=(pltpu.VMEM(...]
    unnamed x2, local copies, waits for them, and re-layouts: 2.67 us -> 1.22 us
where the time goes in v3:
time: 35 us; the launch traced here: 34.8 us
  Pallas kernels  33 us (94%)
  local copies, waits for them, and re-layouts  1.22 us (3%)
  between operations  0.64 us (2%)
    pallas_call x1, Pallas kernels, body(): pl.pallas_call(functools.partial(run_step, sizes), out_shape=(pltpu.VMEM(...  33 us
    unnamed x2, local copies, waits for them, and re-layouts  1.22 us

profile of v3, /device:TPU:0, one launch (start us, length us, event | category | flops | bytes accessed | tf_op | source)
XLA Modules:
  0.0 34.8 jit_solution(14621490099140185472)
XLA Ops:
  0.6 33.0 %step.1 = (f32[32,256]{1,0:T(8,128)S(1)}, f32[1,2048]{1,0:T(1,128)S(1)}) custom-call(s32[16,1024]{1,0:T(8,128)} %bitcast.8, s32[1,1024]{1,0:T(1,128)} %lengths_in.1, bf16[32768,128]{1,0:T(8,128)(2,1)} %bitcast.7, bf16[2048,256]{1,0:T(8,128)(2,1)} %weight_in.1, bf16[2048,512]{1,0:T(8,128)(2,1)} %features_in.1, bf16[512,1024]{1,0:T(8,128)(2,1)} %w1_in.1, ...), custom_call_target="tpu_custom_call" | custom-call | tf_op jit(solution)/shard_map/step/pallas_call | solution.py:367
  33.6 0.6 %copy.12 = f32[32,256]{1,0:T(8,128)} copy(f32[32,256]{1,0:T(8,128)S(1)} %get-tuple-element.6) | data formatting | bytes 65536
  34.2 0.6 %copy.13 = f32[2048]{0:T(1024)} copy(f32[2048]{0:T(1024)S(1)} %bitcast.6) | data formatting | bytes 16384

commit v4 on v3

--- a/solution.py
+++ b/solution.py
@@ -57,6 +57,7 @@
     positives,
     pooled,
     arrived,
+    helped,
     joined,
     user_hi,
     user_lo,
@@ -74,6 +75,7 @@
     send_c,
     recv_c,
     ready,
+    recv_x,
     *index,
 ):
     num_tab, num_cand, num_dp = sizes
@@ -98,8 +100,20 @@
     items_step = items // steps
     columns = items // LANES
 
+    paired = num_tab == 2 and num_cand == 4 and num_dp % 2 == 0 and blocks_step == 1
+    given_end = slots
+    kept_start = slots + GAP
+    kept_end = kept_start + slots
+    far = lax.rem(c + lax.div(num_cand, 2), num_cand)
+    mirror = num_cand - 1 - c
+    near = c + 1 - 2 * lax.rem(c, 2)
+
     def place(index):
-        return (index // groups, index // num_dp % num_cand, index % num_dp)
+        return (
+            lax.div(index, groups),
+            lax.rem(lax.div(index, num_dp), num_cand),
+            lax.rem(index, num_dp),
+        )
 
     barrier = pltpu.get_barrier_semaphore()
 
@@ -123,7 +137,7 @@
         return pltpu.make_async_copy(table.at[part], narrow.at[lax.rem(n, held)], table_sems.at[n])
 
     def in_plane(slot):
-        return (slot // num_dp, c, slot % num_dp)
+        return (lax.div(slot, num_dp), c, lax.rem(slot, num_dp))
 
     for load in loads[:2]:
         load.start()
@@ -133,13 +147,15 @@
         peer = (t, lax.rem(c + j, num_cand), d)
         pl.semaphore_signal(barrier, inc=1, device_id=peer, device_id_type=MESH)
 
+    for n in range(min(chunks, held)):
+        chunk_copy(n).start()
+
     @pl.loop(1, slots)
     def _(j):
         peer = in_plane(lax.rem(my_slot + j, slots))
         pl.semaphore_signal(barrier, inc=1, device_id=peer, device_id_type=MESH)
 
-    for n in range(min(chunks, held)):
-        chunk_copy(n).start()
+    helped[slots] = jnp.zeros(helped.shape[1:], F32)
     wide[pl.ds(rows, ZERO_ROWS), :] = jnp.zeros((ZERO_ROWS, width), F32)
     for load in loads[:2]:
         load.wait()
@@ -188,10 +204,10 @@
     for copy in index_copies:
         copy.wait()
 
-    def send(dest):
+    def send(dest, slot):
         pltpu.make_async_remote_copy(
             src_ref=pooled.at[dest],
-            dst_ref=arrived.at[me],
+            dst_ref=arrived.at[slot],
             send_sem=send_a,
             recv_sem=recv_a,
             device_id=place(dest),
@@ -199,48 +215,112 @@
         ).start()
 
     def group_at(s):
-        if blocks_step > 1 or num_cand != 4:
-            return lax.rem(me // blocks_step + 1 + s, steps)
-        turn = s // slots
+        if not paired:
+            return lax.rem(lax.div(me, blocks_step) + 1 + s, steps)
+        i, j = turn_of(s)
+        crossing = (s < given_end) | ((s >= kept_start) & (s < kept_end))
+        k = lax.rem(j, slots)
+        r = lax.rem(k, num_dp)
+        pairs = num_dp // 2
+        row = lax.rem(lax.div(d, 2) + pairs - 1 - lax.div(r, 2), pairs)
+        close = row * 2 + lax.rem(d + 1 + r, 2)
+        tab = jnp.where(
+            crossing, jnp.where(s < given_end, 1 - t, t), jnp.where(k < num_dp, 1 - t, t)
+        )
+        dp = jnp.where(crossing, lax.rem(d + 1 + i, num_dp), close)
         plane = jnp.where(
-            turn == 0,
-            (c + 2) % 4,
-            jnp.where(turn == 1, 3 - c, jnp.where(turn == 2, c + 1 - c % 2 * 2, c)),
+            crossing,
+            jnp.where(i < num_dp, far, mirror),
+            jnp.where(j < slots, near, c),
         )
-        slot = lax.rem(my_slot + 1 + s, slots)
-        return (slot // num_dp * num_cand + plane) * num_dp + slot % num_dp
-
-    @pl.loop(0, steps)
-    def _(s):
+        return (tab * num_cand + plane) * num_dp + dp
+
+    def turn_of(s):
+        i = jnp.where(s < given_end, s, s - kept_start)
+        j = s - jnp.where(s < kept_start, given_end, slots * 2)
+        return i, j
+
+    def send_group(s, group):
+        if not paired:
+            for i in range(blocks_step):
+                send(group * blocks_step + i, me)
+            return
+        i, j = turn_of(s)
+
+        @pl.when(s < given_end)
+        def _():
+            pltpu.make_async_remote_copy(
+                src_ref=pooled.at[group],
+                dst_ref=helped.at[i],
+                send_sem=send_a,
+                recv_sem=recv_x.at[i],
+                device_id=(1 - t, c, d),
+                device_id_type=MESH,
+            ).start()
+
+        @pl.when(s >= given_end)
+        def _():
+            kept = lax.div(i, num_dp) * num_dp + d
+            direct = slots + jnp.where(j < slots, 0, slots) + my_slot
+            send(group, jnp.where((s >= kept_start) & (s < kept_end), kept, direct))
+
+    def gather(s, groups_then_now):
+        before, groups_now = groups_then_now
+
         @pl.when(s == 1)
         def _():
             pl.semaphore_wait(ready, slots - 1)
 
         @pl.when(s > 0)
         def _():
-            before = group_at(s - 1)
-            for i in range(blocks_step):
-                send(before * blocks_step + i)
-
-        group = group_at(s)
-        first = group * items_step
-        for k in range(items_step):
-            terms = [wide[pl.ds(of_place[first + k], 1), :] for of_place in index]
-            while len(terms) > 1:
-                terms = [a + b for a, b in zip(terms[::2], terms[1::2])] + (
-                    [terms[-1]] if len(terms) % 2 else []
-                )
-            row = terms[0] * inverse[pl.ds(first + k, 1), :]
-            pooled[group * blocks_step + k // per_block, pl.ds(k % per_block, 1), :] = row
-
-    last = group_at(steps - 1)
+            for i in range(AT_ONCE):
+                send_group(s * AT_ONCE - AT_ONCE + i, before[i])
+
+        if paired:
+
+            @pl.when((s * AT_ONCE >= kept_start) & (s * AT_ONCE < kept_end))
+            def _():
+                for i in range(AT_ONCE):
+                    block = helped.at[s * AT_ONCE + i - kept_start]
+                    pltpu.make_async_copy(
+                        block, block, recv_x.at[s * AT_ONCE + i - kept_start]
+                    ).wait()
+
+        for i in range(AT_ONCE):
+            now = s * AT_ONCE + i
+            group = groups_now[i]
+            first = group * items_step
+            if paired:
+                keeps = (now >= kept_start) & (now < kept_end)
+                help_at = jnp.where(keeps, now - kept_start, slots)
+            for k in range(items_step):
+                terms = [wide[pl.ds(of_place[first + k], 1), :] for of_place in index]
+                while len(terms) > 1:
+                    terms = [a + b for a, b in zip(terms[::2], terms[1::2])] + (
+                        [terms[-1]] if len(terms) % 2 else []
+                    )
+                row = terms[0] * inverse[pl.ds(first + k, 1), :]
+                if paired:
+                    row = row + helped[help_at, pl.ds(k, 1), :]
+                pooled[group * blocks_step + k // per_block, pl.ds(k % per_block, 1), :] = row
+
+        return groups_now, groups_of(s + 1)
+
+    def groups_of(s):
+        return tuple(group_at(s * AT_ONCE + i) for i in range(AT_ONCE))
+
+    start = groups_of(jnp.int32(0))
+    finish, _ = lax.fori_loop(0, steps // AT_ONCE, gather, (start, start))
+    for i in range(AT_ONCE - 1):
+        send_group(jnp.int32(steps - AT_ONCE + i), finish[i])
+    last = finish[AT_ONCE - 1]
     for i in range(blocks_step):
         dest = last * blocks_step + i
         if blocks_step > 1:
 
             @pl.when(dest != me)
             def _():
-                send(dest)
+                send(dest, me)
 
     for load in loads[2:]:
         load.wait()
@@ -264,14 +344,27 @@
     early = tiles * EARLY // 8
     pl.loop(0, early)(tower)
 
-    arrived[me] = pooled[me]
+    arrived[slots * 2 + my_slot if paired else me] = pooled[me]
     others = pl.ds(0, total - 1)
-    pltpu.make_async_copy(arrived.at[others], arrived.at[others], recv_a).wait()
-    for f in range(groups):
-        block = arrived[f]
-        for s in range(1, num_tab):
-            block = block + arrived[s * groups + f]
-        joined[:, f * width : (f + 1) * width] = block
+    landed = pl.ds(0, slots * 3 - 1 if paired else total - 1)
+    pltpu.make_async_copy(arrived.at[landed], arrived.at[landed], recv_a).wait()
+
+    def join(table, block):
+        columns = pl.ds(pl.multiple_of(table * width, width), width)
+        joined[:, columns] = block
+
+    if paired:
+        for f in range(num_dp):
+            join(far * num_dp + f, arrived[f])
+            join(mirror * num_dp + f, arrived[num_dp + f])
+            for at, plane in ((slots, near), (slots * 2, c)):
+                join(plane * num_dp + f, arrived[at + f] + arrived[at + num_dp + f])
+    else:
+        for f in range(groups):
+            block = arrived[f]
+            for s in range(1, num_tab):
+                block = block + arrived[s * groups + f]
+            join(f, block)
     hi, lo = split2(joined[...])
     both = dot(jnp.concatenate([hi, lo], axis=0), weight[...])
     item_emb = unit_rows(both[:per_block] + both[per_block:])
@@ -317,9 +410,8 @@
             jnp.where(ids == positives[:, rows], scores, jnp.float32(0.0)), axis=0, keepdims=True
         )
 
-    @pl.loop(1, num_cand)
-    def _(j):
-        peer = lax.rem(c + j, num_cand)
+    for j in range(1, num_cand):
+        peer = (mirror, far, near)[j - 1] if num_cand == 4 else lax.rem(c + j, num_cand)
         pltpu.make_async_remote_copy(
             src_ref=sums_here,
             dst_ref=sums_all.at[c],
@@ -344,6 +436,8 @@
 
 TILE = 512
 EARLY = 2
+AT_ONCE = 2
+GAP = 2
 COLUMN = 512
 
 
@@ -386,6 +480,7 @@
             pltpu.VMEM((1, users), jnp.int32),
             pltpu.VMEM((total, per_block, width), F32),
             pltpu.VMEM((total, per_block, width), F32),
+            pltpu.VMEM((slots + 1, per_block, width), F32),
             pltpu.VMEM((per_block, item_weight.shape[0]), F32),
             pltpu.VMEM((users, embed), BF16),
             pltpu.VMEM((users, embed), BF16),
@@ -398,7 +493,7 @@
             pltpu.SemaphoreType.DMA((length,)),
         ]
         + [pltpu.SemaphoreType.DMA] * 6
-        + [pltpu.SemaphoreType.REGULAR]
+        + [pltpu.SemaphoreType.REGULAR, pltpu.SemaphoreType.DMA((slots,))]
         + [pltpu.SMEM((items,), jnp.int32)] * length,
         compiler_params=pltpu.CompilerParams(
             collective_id=0, has_side_effects=True, vmem_limit_bytes=VMEM_LIMIT

time: 35 us -> 34.1 us (0.974)
  Pallas kernels: 33 us -> 32.1 us
    pallas_call x1, Pallas kernels: 33 us -> 32.1 us  [body(): pl.pallas_call(functools.partial(run_step, sizes), out_shape=(pltpu.VMEM(...]
where the time goes in v4:
time: 34.1 us; the launch traced here: 34 us
  Pallas kernels  32.1 us (94%)
  local copies, waits for them, and re-layouts  1.22 us (4%)
  between operations  0.64 us (2%)
    pallas_call x1, Pallas kernels, body(): pl.pallas_call(functools.partial(run_step, sizes), out_shape=(pltpu.VMEM(...  32.1 us
    unnamed x2, local copies, waits for them, and re-layouts  1.22 us

profile of v4, /device:TPU:0, one launch (start us, length us, event | category | flops | bytes accessed | tf_op | source)
XLA Modules:
  0.0 34.0 jit_solution(3770517032045603956)
XLA Ops:
  0.6 32.1 %step.1 = (f32[32,256]{1,0:T(8,128)S(1)}, f32[1,2048]{1,0:T(1,128)S(1)}) custom-call(s32[16,1024]{1,0:T(8,128)} %bitcast.8, s32[1,1024]{1,0:T(1,128)} %lengths_in.1, bf16[32768,128]{1,0:T(8,128)(2,1)} %bitcast.7, bf16[2048,256]{1,0:T(8,128)(2,1)} %weight_in.1, bf16[2048,512]{1,0:T(8,128)(2,1)} %features_in.1, bf16[512,1024]{1,0:T(8,128)(2,1)} %w1_in.1, ...), custom_call_target="tpu_custom_call" | custom-call | tf_op jit(solution)/shard_map/step/pallas_call | solution.py:461
  32.8 0.6 %copy.12 = f32[32,256]{1,0:T(8,128)} copy(f32[32,256]{1,0:T(8,128)S(1)} %get-tuple-element.6) | data formatting | bytes 65536
  33.4 0.6 %copy.13 = f32[2048]{0:T(1024)} copy(f32[2048]{0:T(1024)S(1)} %bitcast.6) | data formatting | bytes 16384

commit v5 on v4

--- a/solution.py
+++ b/solution.py
@@ -214,20 +214,24 @@
             device_id_type=MESH,
         ).start()
 
+    def plane_slot(k):
+        r = lax.rem(k, num_dp)
+        pairs = num_dp // 2
+        row = lax.rem(lax.div(d, 2) + pairs - 1 - lax.div(r, 2), pairs)
+        tab = jnp.where(k < num_dp, 1 - t, t)
+        return tab * num_dp + row * 2 + lax.rem(d + 1 + r, 2)
+
     def group_at(s):
         if not paired:
             return lax.rem(lax.div(me, blocks_step) + 1 + s, steps)
         i, j = turn_of(s)
         crossing = (s < given_end) | ((s >= kept_start) & (s < kept_end))
         k = lax.rem(j, slots)
-        r = lax.rem(k, num_dp)
-        pairs = num_dp // 2
-        row = lax.rem(lax.div(d, 2) + pairs - 1 - lax.div(r, 2), pairs)
-        close = row * 2 + lax.rem(d + 1 + r, 2)
+        close = plane_slot(k)
         tab = jnp.where(
-            crossing, jnp.where(s < given_end, 1 - t, t), jnp.where(k < num_dp, 1 - t, t)
+            crossing, jnp.where(s < given_end, 1 - t, t), lax.div(close, num_dp)
         )
-        dp = jnp.where(crossing, lax.rem(d + 1 + i, num_dp), close)
+        dp = lax.rem(jnp.where(crossing, d + 1 + i, close), num_dp)
         plane = jnp.where(
             crossing,
             jnp.where(i < num_dp, far, mirror),
@@ -370,9 +374,9 @@
     item_emb = unit_rows(both[:per_block] + both[per_block:])
     emb_out[...] = item_emb
 
-    @pl.loop(1, slots)
-    def _(j):
-        slot = lax.rem(my_slot + j, slots)
+    @pl.loop(0, slots - 1)
+    def _(k):
+        slot = plane_slot(k) if paired else lax.rem(my_slot + 1 + k, slots)
         pltpu.make_async_remote_copy(
             src_ref=emb_out,
             dst_ref=gathered.at[my_slot],
@@ -438,7 +442,16 @@
 EARLY = 2
 AT_ONCE = 2
 GAP = 2
-COLUMN = 512
+COLUMN = 2048
+
+
+def keep(emb_in, loss_in, emb_out, loss_out, sems):
+    pairs = ((emb_in, emb_out), (loss_in, loss_out))
+    copies = [pltpu.make_async_copy(a, b, sems.at[i]) for i, (a, b) in enumerate(pairs)]
+    for copy in copies:
+        copy.start()
+    for copy in copies:
+        copy.wait()
 
 
 def body(
@@ -456,7 +469,7 @@
     chunk = min(rows, 4096)
     chunks = rows // chunk
     held = min(chunks, 8)
-    far = pl.BlockSpec(memory_space=pltpu.HBM)
+    anywhere = pl.BlockSpec(memory_space=pl.ANY)
     near = pl.BlockSpec(memory_space=pltpu.VMEM)
     item_emb, loss = pl.pallas_call(
         functools.partial(run_step, sizes),
@@ -464,7 +477,7 @@
             pltpu.VMEM((per_block, embed), F32),
             pltpu.VMEM((1, users), F32),
         ),
-        in_specs=[far] * 8,
+        in_specs=[anywhere] * 8,
         out_specs=(near, near),
         scratch_shapes=[
             pltpu.VMEM((length, items), jnp.int32),
@@ -509,6 +522,17 @@
         user_w2,
         positive_items[None, :],
     )
+    item_emb, loss = pl.pallas_call(
+        keep,
+        out_shape=(
+            jax.ShapeDtypeStruct((per_block, embed), F32),
+            jax.ShapeDtypeStruct((1, users), F32),
+        ),
+        in_specs=[pl.BlockSpec(memory_space=pltpu.VMEM)] * 2,
+        out_specs=(anywhere, anywhere),
+        scratch_shapes=[pltpu.SemaphoreType.DMA((2,))],
+        name="keep",
+    )(*[pltpu.with_memory_space_constraint(x, pltpu.VMEM) for x in (item_emb, loss)])
     return (item_emb, loss[0])
 
 

time: 34.1 us -> 32.9 us (0.965)
  local copies, waits for them, and re-layouts: 1.22 us -> 0 us
    unnamed x2 -> x0, local copies, waits for them, and re-layouts: 1.22 us -> none
    pallas_call x1, Pallas kernels: 32.1 us -> 31.5 us  [body(): pl.pallas_call(functools.partial(run_step, sizes), out_shape=(pltpu.VMEM(...]
    pallas_call x0 -> x1, Pallas kernels: none -> 0.64 us  [body(): pl.pallas_call(keep, out_shape=(jax.ShapeDtypeStruct((per_block, embed),...]
where the time goes in v5:
time: 32.9 us; the launch traced here: 32.8 us
  Pallas kernels  32.1 us (98%)
  between operations  0.64 us (2%)
    pallas_call x1, Pallas kernels, body(): pl.pallas_call(functools.partial(run_step, sizes), out_shape=(pltpu.VMEM(...  31.5 us

profile of v5, /device:TPU:0, one launch (start us, length us, event | category | flops | bytes accessed | tf_op | source)
XLA Modules:
  0.0 32.8 jit_solution(5317320061396489881)
XLA Ops:
  0.6 31.5 %step.1 = (f32[32,256]{1,0:T(8,128)S(1)}, f32[1,2048]{1,0:T(1,128)S(1)}) custom-call(s32[16,1024]{1,0:T(8,128)} %bitcast.7, s32[1,1024]{1,0:T(1,128)} %lengths_in.1, bf16[32768,128]{1,0:T(8,128)(2,1)} %bitcast.6, bf16[2048,256]{1,0:T(8,128)(2,1)} %weight_in.1, bf16[2048,512]{1,0:T(8,128)(2,1)} %features_in.1, bf16[512,1024]{1,0:T(8,128)(2,1)} %w1_in.1, ...), custom_call_target="tpu_custom_call" | custom-call | tf_op jit(solution)/shard_map/step/pallas_call | solution.py:474
  32.1 0.6 %keep.1 = (f32[32,256]{1,0:T(8,128)}, f32[1,2048]{1,0:T(1,128)}) custom-call(f32[32,256]{1,0:T(8,128)S(1)} %get-tuple-element.6.emb_in, f32[1,2048]{1,0:T(1,128)S(1)} %get-tuple-element.7.loss_in), custom_call_target="tpu_custom_call" | custom-call | tf_op jit(solution)/shard_map/keep/pallas_call | solution.py:525

commit v6 on v5

--- a/solution.py
+++ b/solution.py
@@ -58,7 +58,6 @@
     pooled,
     arrived,
     helped,
-    joined,
     user_hi,
     user_lo,
     gathered,
@@ -100,7 +99,7 @@
     items_step = items // steps
     columns = items // LANES
 
-    paired = num_tab == 2 and num_cand == 4 and num_dp % 2 == 0 and blocks_step == 1
+    paired = num_tab == 2 and num_cand == 4 and num_dp == 4 and blocks_step == 1
     given_end = slots
     kept_start = slots + GAP
     kept_end = kept_start + slots
@@ -209,25 +208,31 @@
             src_ref=pooled.at[dest],
             dst_ref=arrived.at[slot],
             send_sem=send_a,
-            recv_sem=recv_a,
+            recv_sem=recv_a.at[0],
             device_id=place(dest),
             device_id_type=MESH,
         ).start()
 
     def plane_slot(k):
-        r = lax.rem(k, num_dp)
-        pairs = num_dp // 2
-        row = lax.rem(lax.div(d, 2) + pairs - 1 - lax.div(r, 2), pairs)
-        tab = jnp.where(k < num_dp, 1 - t, t)
-        return tab * num_dp + row * 2 + lax.rem(d + 1 + r, 2)
-
-    def group_at(s):
+        outer = k < num_tab
+        inner = k >= num_tab + num_dp
+        even = lax.rem(k, 2) == 0
+        over_tab = outer | (even & ~inner)
+        over_row = outer | (~even & ~inner)
+        shift = jnp.where(outer | inner, k + 1, lax.div(k, 2))
+        tab = jnp.where(over_tab, 1 - t, t)
+        row = lax.div(d, 2)
+        row = jnp.where(over_row, 1 - row, row)
+        return tab * num_dp + row * 2 + lax.rem(d + shift, 2)
+
+    def block_at(s):
         if not paired:
-            return lax.rem(lax.div(me, blocks_step) + 1 + s, steps)
-        i, j = turn_of(s)
+            group = lax.rem(lax.div(me, blocks_step) + 1 + s, steps)
+            return (group,)
+        i = jnp.where(s < given_end, s, s - kept_start)
+        j = s - jnp.where(s < kept_start, given_end, slots * 2)
+        close = plane_slot(lax.rem(j, slots))
         crossing = (s < given_end) | ((s >= kept_start) & (s < kept_end))
-        k = lax.rem(j, slots)
-        close = plane_slot(k)
         tab = jnp.where(
             crossing, jnp.where(s < given_end, 1 - t, t), lax.div(close, num_dp)
         )
@@ -237,62 +242,71 @@
             jnp.where(i < num_dp, far, mirror),
             jnp.where(j < slots, near, c),
         )
-        return (tab * num_cand + plane) * num_dp + dp
-
-    def turn_of(s):
-        i = jnp.where(s < given_end, s, s - kept_start)
-        j = s - jnp.where(s < kept_start, given_end, slots * 2)
-        return i, j
-
-    def send_group(s, group):
+        kept = jnp.where(i < num_dp, 0, num_dp) + d
+        direct = jnp.where(j < slots, slots, slots * 2) + my_slot
+        target = jnp.where(crossing, jnp.where(s < given_end, i, kept), direct)
+        return ((tab * num_cand + plane) * num_dp + dp, tab, plane, dp, target)
+
+    def send_block(s, block, given):
         if not paired:
             for i in range(blocks_step):
-                send(group * blocks_step + i, me)
+                send(block[0] * blocks_step + i, me)
             return
-        i, j = turn_of(s)
-
-        @pl.when(s < given_end)
-        def _():
-            pltpu.make_async_remote_copy(
-                src_ref=pooled.at[group],
-                dst_ref=helped.at[i],
-                send_sem=send_a,
-                recv_sem=recv_x.at[i],
-                device_id=(1 - t, c, d),
-                device_id_type=MESH,
-            ).start()
-
-        @pl.when(s >= given_end)
-        def _():
-            kept = lax.div(i, num_dp) * num_dp + d
-            direct = slots + jnp.where(j < slots, 0, slots) + my_slot
-            send(group, jnp.where((s >= kept_start) & (s < kept_end), kept, direct))
+        group, tab, plane, dp, target = block
+        if given:
+            arrival = helped.at[target], recv_x.at[target], (1 - t, c, d)
+        else:
+            keeps = (s >= kept_start) & (s < kept_end)
+            arrival = arrived.at[target], recv_a.at[jnp.where(keeps, 1, 0)], (tab, plane, dp)
+        pltpu.make_async_remote_copy(
+            src_ref=pooled.at[group],
+            dst_ref=arrival[0],
+            send_sem=send_a,
+            recv_sem=arrival[1],
+            device_id=arrival[2],
+            device_id_type=MESH,
+        ).start()
 
     def gather(s, groups_then_now):
         before, groups_now = groups_then_now
 
-        @pl.when(s == 1)
-        def _():
-            pl.semaphore_wait(ready, slots - 1)
-
-        @pl.when(s > 0)
-        def _():
+        def sends(given):
             for i in range(AT_ONCE):
-                send_group(s * AT_ONCE - AT_ONCE + i, before[i])
+                send_block(s * AT_ONCE - AT_ONCE + i, before[i], given)
 
         if paired:
+
+            @pl.when((s > 0) & (s * AT_ONCE <= given_end))
+            def _():
+                @pl.when(s == 1)
+                def _():
+                    pl.semaphore_wait(ready, slots - 1)
+
+                sends(True)
+
+            @pl.when(s * AT_ONCE > given_end)
+            def _():
+                sends(False)
 
             @pl.when((s * AT_ONCE >= kept_start) & (s * AT_ONCE < kept_end))
             def _():
                 for i in range(AT_ONCE):
-                    block = helped.at[s * AT_ONCE + i - kept_start]
-                    pltpu.make_async_copy(
-                        block, block, recv_x.at[s * AT_ONCE + i - kept_start]
-                    ).wait()
+                    at = s * AT_ONCE + i - kept_start
+                    block = helped.at[at]
+                    pltpu.make_async_copy(block, block, recv_x.at[at]).wait()
+        else:
+
+            @pl.when(s > 0)
+            def _():
+                @pl.when(s == 1)
+                def _():
+                    pl.semaphore_wait(ready, slots - 1)
+
+                sends(False)
 
         for i in range(AT_ONCE):
             now = s * AT_ONCE + i
-            group = groups_now[i]
+            group = groups_now[i][0]
             first = group * items_step
             if paired:
                 keeps = (now >= kept_start) & (now < kept_end)
@@ -311,13 +325,13 @@
         return groups_now, groups_of(s + 1)
 
     def groups_of(s):
-        return tuple(group_at(s * AT_ONCE + i) for i in range(AT_ONCE))
+        return tuple(block_at(s * AT_ONCE + i) for i in range(AT_ONCE))
 
     start = groups_of(jnp.int32(0))
     finish, _ = lax.fori_loop(0, steps // AT_ONCE, gather, (start, start))
     for i in range(AT_ONCE - 1):
-        send_group(jnp.int32(steps - AT_ONCE + i), finish[i])
-    last = finish[AT_ONCE - 1]
+        send_block(jnp.int32(steps - AT_ONCE + i), finish[i], False)
+    last = finish[AT_ONCE - 1][0]
     for i in range(blocks_step):
         dest = last * blocks_step + i
         if blocks_step > 1:
@@ -348,30 +362,49 @@
     early = tiles * EARLY // 8
     pl.loop(0, early)(tower)
 
-    arrived[slots * 2 + my_slot if paired else me] = pooled[me]
     others = pl.ds(0, total - 1)
-    landed = pl.ds(0, slots * 3 - 1 if paired else total - 1)
-    pltpu.make_async_copy(arrived.at[landed], arrived.at[landed], recv_a).wait()
-
-    def join(table, block):
-        columns = pl.ds(pl.multiple_of(table * width, width), width)
-        joined[:, columns] = block
+
+    def wait_blocks(first, number, kind):
+        blocks = arrived.at[pl.ds(first, number)]
+        pltpu.make_async_copy(blocks, blocks, recv_a.at[kind]).wait()
+
+    def project(planes):
+        depth = num_dp * width
+        result = None
+        for plane, blocks in planes:
+            part = jnp.concatenate(split2(jnp.concatenate(blocks, axis=1)), axis=0)
+            at = pl.ds(pl.multiple_of(plane * depth, depth), depth)
+            term = dot(part, weight[at, :])
+            result = term if result is None else result + term
+        return result[:per_block] + result[per_block:]
 
     if paired:
-        for f in range(num_dp):
-            join(far * num_dp + f, arrived[f])
-            join(mirror * num_dp + f, arrived[num_dp + f])
-            for at, plane in ((slots, near), (slots * 2, c)):
-                join(plane * num_dp + f, arrived[at + f] + arrived[at + num_dp + f])
+        wait_blocks(0, slots, 1)
+        crossed = project(
+            (plane, [arrived[at + f] for f in range(num_dp)])
+            for plane, at in ((far, 0), (mirror, num_dp))
+        )
+        arrived[slots * 2 + my_slot] = pooled[me]
+        wait_blocks(slots, slots * 2 - 1, 0)
+        item_pre = crossed + project(
+            (plane, [arrived[at + f] + arrived[at + num_dp + f] for f in range(num_dp)])
+            for plane, at in ((near, slots), (c, slots * 2))
+        )
     else:
-        for f in range(groups):
+        arrived[me] = pooled[me]
+        wait_blocks(0, total - 1, 0)
+
+        def table_block(f):
             block = arrived[f]
             for s in range(1, num_tab):
                 block = block + arrived[s * groups + f]
-            join(f, block)
-    hi, lo = split2(joined[...])
-    both = dot(jnp.concatenate([hi, lo], axis=0), weight[...])
-    item_emb = unit_rows(both[:per_block] + both[per_block:])
+            return block
+
+        item_pre = project(
+            (plane, [table_block(plane * num_dp + f) for f in range(num_dp)])
+            for plane in range(num_cand)
+        )
+    item_emb = unit_rows(item_pre)
     emb_out[...] = item_emb
 
     @pl.loop(0, slots - 1)
@@ -494,7 +527,6 @@
             pltpu.VMEM((total, per_block, width), F32),
             pltpu.VMEM((total, per_block, width), F32),
             pltpu.VMEM((slots + 1, per_block, width), F32),
-            pltpu.VMEM((per_block, item_weight.shape[0]), F32),
             pltpu.VMEM((users, embed), BF16),
             pltpu.VMEM((users, embed), BF16),
             pltpu.VMEM((slots, per_block, embed), F32),
@@ -505,7 +537,8 @@
             pltpu.SemaphoreType.DMA((chunks,)),
             pltpu.SemaphoreType.DMA((length,)),
         ]
-        + [pltpu.SemaphoreType.DMA] * 6
+        + [pltpu.SemaphoreType.DMA, pltpu.SemaphoreType.DMA((2,))]
+        + [pltpu.SemaphoreType.DMA] * 4
         + [pltpu.SemaphoreType.REGULAR, pltpu.SemaphoreType.DMA((slots,))]
         + [pltpu.SMEM((items,), jnp.int32)] * length,
         compiler_params=pltpu.CompilerParams(

time: 32.9 us -> 32.6 us (level)
    pallas_call x1, Pallas kernels: 31.5 us -> 31.1 us  [body(): pl.pallas_call(functools.partial(run_step, sizes), out_shape=(pltpu.VMEM(...]
where the time goes in v6:
time: 32.6 us; the launch traced here: 32.4 us
  Pallas kernels  31.8 us (98%)
  between operations  0.64 us (2%)
    pallas_call x1, Pallas kernels, body(): pl.pallas_call(functools.partial(run_step, sizes), out_shape=(pltpu.VMEM(...  31.1 us

profile of v6, /device:TPU:0, one launch (start us, length us, event | category | flops | bytes accessed | tf_op | source)
XLA Modules:
  0.0 32.4 jit_solution(9645095716365309104)
XLA Ops:
  0.6 31.1 %step.1 = (f32[32,256]{1,0:T(8,128)S(1)}, f32[1,2048]{1,0:T(1,128)S(1)}) custom-call(s32[16,1024]{1,0:T(8,128)} %bitcast.7, s32[1,1024]{1,0:T(1,128)} %lengths_in.1, bf16[32768,128]{1,0:T(8,128)(2,1)} %bitcast.6, bf16[2048,256]{1,0:T(8,128)(2,1)} %weight_in.1, bf16[2048,512]{1,0:T(8,128)(2,1)} %features_in.1, bf16[512,1024]{1,0:T(8,128)(2,1)} %w1_in.1, ...), custom_call_target="tpu_custom_call" | custom-call | tf_op jit(solution)/shard_map/step/pallas_call | solution.py:507
  31.8 0.6 %keep.1 = (f32[32,256]{1,0:T(8,128)}, f32[1,2048]{1,0:T(1,128)}) custom-call(f32[32,256]{1,0:T(8,128)S(1)} %get-tuple-element.6.emb_in, f32[1,2048]{1,0:T(1,128)S(1)} %get-tuple-element.7.loss_in), custom_call_target="tpu_custom_call" | custom-call | tf_op jit(solution)/shard_map/keep/pallas_call | solution.py:558

commit v7 on v6

--- a/solution.py
+++ b/solution.py
@@ -474,7 +474,7 @@
 TILE = 512
 EARLY = 2
 AT_ONCE = 2
-GAP = 2
+GAP = 6
 COLUMN = 2048
 
 

time: 32.6 us -> 32.1 us (0.985)
  Pallas kernels: 31.8 us -> 31.3 us
    pallas_call x1, Pallas kernels: 31.1 us -> 30.7 us  [body(): pl.pallas_call(functools.partial(run_step, sizes), out_shape=(pltpu.VMEM(...]
where the time goes in v7:
time: 32.1 us; the launch traced here: 32 us
  Pallas kernels  31.3 us (98%)
  between operations  0.64 us (2%)
    pallas_call x1, Pallas kernels, body(): pl.pallas_call(functools.partial(run_step, sizes), out_shape=(pltpu.VMEM(...  30.7 us

profile of v7, /device:TPU:0, one launch (start us, length us, event | category | flops | bytes accessed | tf_op | source)
XLA Modules:
  0.0 32.0 jit_solution(7121726574177624215)
XLA Ops:
  0.6 30.7 %step.1 = (f32[32,256]{1,0:T(8,128)S(1)}, f32[1,2048]{1,0:T(1,128)S(1)}) custom-call(s32[16,1024]{1,0:T(8,128)} %bitcast.7, s32[1,1024]{1,0:T(1,128)} %lengths_in.1, bf16[32768,128]{1,0:T(8,128)(2,1)} %bitcast.6, bf16[2048,256]{1,0:T(8,128)(2,1)} %weight_in.1, bf16[2048,512]{1,0:T(8,128)(2,1)} %features_in.1, bf16[512,1024]{1,0:T(8,128)(2,1)} %w1_in.1, ...), custom_call_target="tpu_custom_call" | custom-call | tf_op jit(solution)/shard_map/step/pallas_call | solution.py:507
  31.3 0.6 %keep.1 = (f32[32,256]{1,0:T(8,128)}, f32[1,2048]{1,0:T(1,128)}) custom-call(f32[32,256]{1,0:T(8,128)S(1)} %get-tuple-element.6.emb_in, f32[1,2048]{1,0:T(1,128)S(1)} %get-tuple-element.7.loss_in), custom_call_target="tpu_custom_call" | custom-call | tf_op jit(solution)/shard_map/keep/pallas_call | solution.py:558
